TPU v7x, 32 devices: a 4x4x1 block of a 4x4x8 slice. The times are simulated.
32 devices in a mesh: dp: 1 (over z), gp: 32 (over y, x, core).
Axes of the slice: x: 4, y: 4, z: 1, core: 2. Of those that a mesh axis runs over, the one named last changes fastest.
The devices are a block of a 4x4x8 slice.
Arguments:
- x_prev: float32 [16384, 83], P(('dp', 'gp'))
- x_cur: float32 [16384, 83], P(('dp', 'gp'))
- forcing: float32 [16384, 2, 5], P(('dp', 'gp'))
- grid_static: float32 [16384, 5], P(('dp', 'gp'))
- g2m_feat: float32 [16384, 4], P(('dp', 'gp'))
- m2g_feat: float32 [16384, 4], P(('dp', 'gp'))
- mesh_feat: float32 [4096, 3], P(('dp', 'gp'))
- mesh_edge_feat: float32 [4096, 6, 4], P(('dp', 'gp'))
- norm_stats: float32 [4, 83], replicated
- w_grid_in: bfloat16 [176, 512], replicated
- w_mesh_in: bfloat16 [3, 512], replicated
- w_eemb_in: bfloat16 [3, 4, 512], replicated
- w_embed_out: bfloat16 [5, 512, 512], replicated
- w_edge_in: bfloat16 [18, 1536, 512], replicated
- w_edge_out: bfloat16 [18, 512, 512], replicated
- w_node_in: bfloat16 [18, 1024, 512], replicated
- w_node_out: bfloat16 [18, 512, 512], replicated
- w_grid_self: bfloat16 [2, 512, 512], replicated
- w_out_hidden: bfloat16 [512, 512], replicated
- w_out_final: bfloat16 [512, 83], replicated
Outputs:
- output 1: float32 [16384, 83], P(('dp', 'gp'))
- output 2: float32 [16384, 83], P(('dp', 'gp'))
All inputs are finite; a program needn't handle non-finite values.
Results may differ from a plain program's by a relative error of at most 0.00836121.
Values are sent between devices in bfloat16 or wider.
A program may use at most 768 MiB of HBM per device.

v0:
```python
import jax
import jax.numpy as jnp
from jax import lax
from jax.sharding import PartitionSpec as P


def layer_norm(values):
    centre = jnp.mean(values, axis=-1, keepdims=True)
    centred = values - centre
    spread = jnp.mean(centred * centred, axis=-1, keepdims=True)
    return centred * lax.rsqrt(spread + 1e-5)


def matmul_f32(values, weight):
    return jnp.dot(values, weight, preferred_element_type=jnp.float32)


def mlp_tail(pre_act, w_second):
    hidden = jax.nn.silu(pre_act).astype(jnp.bfloat16)
    return layer_norm(matmul_f32(hidden, w_second))


def residual(base, update):
    return (base.astype(jnp.float32) + update).astype(jnp.bfloat16)


def embed_static(features, w_first, w_second):
    return mlp_tail(matmul_f32(features.astype(jnp.bfloat16), w_first), w_second).astype(jnp.bfloat16)


def solution(mesh):
    group_size = mesh.shape["gp"]
    quarter_hop = group_size // 4
    row_spec = P(("dp", "gp"))
    edge_spec = P(("dp", "gp"), None, None)
    whole = P()

    def shift_pairs(hop_count):
        return [(source, (source + hop_count) % group_size) for source in range(group_size)]

    def local_run(x_prev, x_cur, forcing, grid_static, g2m_feat, m2g_feat, mesh_feat, mesh_edge_feat, norm_stats, w_grid_in, w_mesh_in, w_eemb_in, w_embed_out, w_edge_in, w_edge_out, w_node_in, w_node_out, w_grid_self, w_out_hidden, w_out_final):
        grid_dev = x_prev.shape[0]
        mesh_dev = mesh_feat.shape[0]
        grid_ratio = grid_dev // mesh_dev
        half_shard = mesh_dev // 2
        half_rows = half_shard * grid_ratio
        latent = w_embed_out.shape[-1]
        blocks = w_edge_in.shape[0]
        mesh_lat = embed_static(mesh_feat, w_mesh_in, w_embed_out[1])
        g2m_lat = embed_static(g2m_feat, w_eemb_in[0], w_embed_out[2])
        m2g_lat = embed_static(m2g_feat, w_eemb_in[1], w_embed_out[3])
        edge_base = embed_static(mesh_edge_feat, w_eemb_in[2], w_embed_out[4])
        in_mean = norm_stats[0]
        in_std = norm_stats[1]
        diff_mean = norm_stats[2]
        diff_std = norm_stats[3]
        state_prev = x_prev
        state_cur = x_cur
        outputs = []
        for step_idx in range(2):
            features = jnp.concatenate([(state_prev - in_mean) / in_std, (state_cur - in_mean) / in_std, forcing[:, step_idx, :], grid_static], axis=1)
            grid_lat = embed_static(features, w_grid_in, w_embed_out[0])
            from_prev = lax.ppermute(grid_lat[grid_dev - half_rows:], "gp", shift_pairs(1))
            senders = jnp.concatenate([from_prev, grid_lat[:grid_dev - half_rows]], axis=0)
            w_first = w_edge_in[0]
            recv_term = matmul_f32(mesh_lat, w_first[2 * latent:])
            pre_act = matmul_f32(g2m_lat, w_first[:latent]) + matmul_f32(senders, w_first[latent:2 * latent])
            pre_act = (pre_act.reshape(mesh_dev, grid_ratio, latent) + recv_term[:, None, :]).reshape(grid_dev, latent)
            enc_edge = residual(g2m_lat, mlp_tail(pre_act, w_edge_out[0]))
            enc_sum = jnp.sum(enc_edge.reshape(mesh_dev, grid_ratio, latent), axis=1, dtype=jnp.float32).astype(jnp.bfloat16)
            node_w = w_node_in[0]
            mesh_cur = residual(mesh_lat, mlp_tail(matmul_f32(mesh_lat, node_w[:latent]) + matmul_f32(enc_sum, node_w[latent:]), w_node_out[0]))
            grid_cur = residual(grid_lat, mlp_tail(matmul_f32(grid_lat, w_grid_self[0]), w_grid_self[1]))
            edge_lat = edge_base
            for layer_idx in range(1, blocks - 1):
                prev_tail = lax.ppermute(mesh_cur[mesh_dev - half_shard:], "gp", shift_pairs(1))
                next_head = lax.ppermute(mesh_cur[:half_shard], "gp", shift_pairs(-1))
                far_plus = lax.ppermute(mesh_cur, "gp", shift_pairs(-quarter_hop))
                far_minus = lax.ppermute(mesh_cur, "gp", shift_pairs(quarter_hop))
                w_layer = w_edge_in[layer_idx]
                extended = jnp.concatenate([prev_tail, mesh_cur, next_head, far_plus, far_minus], axis=0)
                send_proj = matmul_f32(extended, w_layer[latent:2 * latent])
                send_term = jnp.stack([
                    send_proj[half_shard + 1:half_shard + 1 + mesh_dev],
                    send_proj[half_shard - 1:half_shard - 1 + mesh_dev],
                    send_proj[2 * half_shard:2 * half_shard + mesh_dev],
                    send_proj[:mesh_dev],
                    send_proj[2 * mesh_dev:3 * mesh_dev],
                    send_proj[3 * mesh_dev:4 * mesh_dev]], axis=1)
                recv_term = matmul_f32(mesh_cur, w_layer[2 * latent:])
                pre_act = jnp.einsum("nkc,cd->nkd", edge_lat, w_layer[:latent], preferred_element_type=jnp.float32) + send_term + recv_term[:, None, :]
                edge_lat = residual(edge_lat, mlp_tail(pre_act, w_edge_out[layer_idx]))
                edge_sum = jnp.sum(edge_lat, axis=1, dtype=jnp.float32).astype(jnp.bfloat16)
                node_w = w_node_in[layer_idx]
                mesh_cur = residual(mesh_cur, mlp_tail(matmul_f32(mesh_cur, node_w[:latent]) + matmul_f32(edge_sum, node_w[latent:]), w_node_out[layer_idx]))
            head_next = lax.ppermute(mesh_cur[:half_shard], "gp", shift_pairs(-1))
            mesh_send = jnp.concatenate([mesh_cur[half_shard:], head_next], axis=0)
            w_last = w_edge_in[blocks - 1]
            send_term = matmul_f32(mesh_send, w_last[latent:2 * latent])
            pre_act = matmul_f32(m2g_lat, w_last[:latent]) + matmul_f32(grid_cur, w_last[2 * latent:])
            pre_act = (pre_act.reshape(mesh_dev, grid_ratio, latent) + send_term[:, None, :]).reshape(grid_dev, latent)
            dec_edge = residual(m2g_lat, mlp_tail(pre_act, w_edge_out[blocks - 1]))
            node_w = w_node_in[blocks - 1]
            grid_out = residual(grid_cur, mlp_tail(matmul_f32(grid_cur, node_w[:latent]) + matmul_f32(dec_edge, node_w[latent:]), w_node_out[blocks - 1]))
            hidden = jax.nn.silu(matmul_f32(grid_out, w_out_hidden)).astype(jnp.bfloat16)
            prediction = matmul_f32(hidden, w_out_final)
            state_next = state_cur + diff_std * prediction + diff_mean
            outputs.append(state_next)
            state_prev, state_cur = state_cur, state_next
        return outputs[0], outputs[1]

    in_specs = (row_spec, row_spec, edge_spec, row_spec, row_spec, row_spec, row_spec, edge_spec, whole) + (whole,) * 11
    return jax.shard_map(local_run, mesh=mesh, in_specs=in_specs, out_specs=(row_spec, row_spec), check_vma=False)
```

profile of v0, /device:TPU:97, one launch (start us, length us, event | category | flops | bytes accessed | tf_op | source)
XLA Modules:
  0.0 1154.3 jit_solution(6253052564023771826)
XLA Ops:
  236.4 6.9 collective-permute-start.22
  273.4 7.1 collective-permute-start.26
  310.6 6.9 collective-permute-start.30
  347.6 6.9 collective-permute-start.34
  384.6 7.1 collective-permute-start.38
  421.8 6.9 collective-permute-start.42
  458.8 6.9 collective-permute-start.46
  495.8 7.3 collective-permute-start.50
  570.2 6.9 collective-permute-start.58
  607.2 7.1 collective-permute-start.62
  698.3 8.5 collective-permute-start.68
  747.8 7.0 collective-permute-start.76
  775.6 7.4 collective-permute-start.80
  803.8 7.0 collective-permute-start.84
  831.5 7.0 collective-permute-start.88
  859.3 7.2 collective-permute-start.92
  887.3 7.0 collective-permute-start.96
  915.1 7.0 collective-permute-start.100
  942.8 7.2 collective-permute-start.104
  970.8 7.0 collective-permute-start.108
  998.6 7.0 collective-permute-start.112
  1026.4 7.3 collective-permute-start.116
  1054.4 7.0 collective-permute-start.120
  1109.9 7.3 collective-permute-start.128
  (1343 shorter events, 978.6 us)
Async XLA Ops:
  8.5 36.5 %collective-permute-start = (bf16[256,512]{0,1:T(8,128)(2,1)}, bf16[256,512]{0,1:T(8,128)(2,1)}, u32[]{:S(2)}, u32[]{:S(2)}) collective-permute-start(bf16[256,512]{0,1:T(8,128)(2,1)} %get-tuple-element.64), channel_id=1, source_target_pairs={{0,1},{1,2},{2,3},{3,4},{4,5},{5,6},{6,7},{7,8},{8,9},{9,10},{10,1... | collective-permute-start | bytes 786440 | tf_op jit(solution)/shard_map/ppermute | solution.py:63
  156.4 14.8 %collective-permute-start.15 = (bf16[128,512]{1,0:T(8,128)(2,1)S(1)}, bf16[128,512]{1,0:T(8,128)(2,1)S(1)}, u32[]{:S(2)}, u32[]{:S(2)}) collective-permute-start(bf16[128,512]{1,0:T(8,128)(2,1)S(1)} %add_convert_fusion.73), channel_id=1, source_target_pairs={{0,24},{1,25},{2,26},{3,27},{4,28},{5,29},{6,30},{7,31},{8,0},{9,1... | collective-permute-start | bytes 393224 | tf_op jit(solution)/shard_map/ppermute | solution.py:78
  193.9 14.4 %collective-permute-start.19 = (bf16[128,512]{1,0:T(8,128)(2,1)S(1)}, bf16[128,512]{1,0:T(8,128)(2,1)S(1)}, u32[]{:S(2)}, u32[]{:S(2)}) collective-permute-start(bf16[128,512]{1,0:T(8,128)(2,1)S(1)} %add_convert_fusion.72), channel_id=1, source_target_pairs={{0,24},{1,25},{2,26},{3,27},{4,28},{5,29},{6,30},{7,31},{8,0},{9,1... | collective-permute-start | bytes 393224 | tf_op jit(solution)/shard_map/ppermute | solution.py:78
  230.8 14.4 %collective-permute-start.23 = (bf16[128,512]{1,0:T(8,128)(2,1)S(1)}, bf16[128,512]{1,0:T(8,128)(2,1)S(1)}, u32[]{:S(2)}, u32[]{:S(2)}) collective-permute-start(bf16[128,512]{1,0:T(8,128)(2,1)S(1)} %add_convert_fusion.71), channel_id=1, source_target_pairs={{0,24},{1,25},{2,26},{3,27},{4,28},{5,29},{6,30},{7,31},{8,0},{9,1... | collective-permute-start | bytes 393224 | tf_op jit(solution)/shard_map/ppermute | solution.py:78
  267.9 14.5 %collective-permute-start.27 = (bf16[128,512]{1,0:T(8,128)(2,1)S(1)}, bf16[128,512]{1,0:T(8,128)(2,1)S(1)}, u32[]{:S(2)}, u32[]{:S(2)}) collective-permute-start(bf16[128,512]{1,0:T(8,128)(2,1)S(1)} %add_convert_fusion.70), channel_id=1, source_target_pairs={{0,24},{1,25},{2,26},{3,27},{4,28},{5,29},{6,30},{7,31},{8,0},{9,1... | collective-permute-start | bytes 393224 | tf_op jit(solution)/shard_map/ppermute | solution.py:78
  269.0 14.1 %collective-permute-start.28 = (bf16[128,512]{1,0:T(8,128)(2,1)S(1)}, bf16[128,512]{1,0:T(8,128)(2,1)S(1)}, u32[]{:S(2)}, u32[]{:S(2)}) collective-permute-start(bf16[128,512]{1,0:T(8,128)(2,1)S(1)} %add_convert_fusion.70), channel_id=1, source_target_pairs={{0,8},{1,9},{2,10},{3,11},{4,12},{5,13},{6,14},{7,15},{8,16},{9,17... | collective-permute-start | bytes 393224 | tf_op jit(solution)/shard_map/ppermute | solution.py:79
  305.0 14.4 %collective-permute-start.31 = (bf16[128,512]{1,0:T(8,128)(2,1)S(1)}, bf16[128,512]{1,0:T(8,128)(2,1)S(1)}, u32[]{:S(2)}, u32[]{:S(2)}) collective-permute-start(bf16[128,512]{1,0:T(8,128)(2,1)S(1)} %add_convert_fusion.69), channel_id=1, source_target_pairs={{0,24},{1,25},{2,26},{3,27},{4,28},{5,29},{6,30},{7,31},{8,0},{9,1... | collective-permute-start | bytes 393224 | tf_op jit(solution)/shard_map/ppermute | solution.py:78
  342.1 14.4 %collective-permute-start.35 = (bf16[128,512]{1,0:T(8,128)(2,1)S(1)}, bf16[128,512]{1,0:T(8,128)(2,1)S(1)}, u32[]{:S(2)}, u32[]{:S(2)}) collective-permute-start(bf16[128,512]{1,0:T(8,128)(2,1)S(1)} %add_convert_fusion.68), channel_id=1, source_target_pairs={{0,24},{1,25},{2,26},{3,27},{4,28},{5,29},{6,30},{7,31},{8,0},{9,1... | collective-permute-start | bytes 393224 | tf_op jit(solution)/shard_map/ppermute | solution.py:78
  379.0 14.6 %collective-permute-start.39 = (bf16[128,512]{1,0:T(8,128)(2,1)S(1)}, bf16[128,512]{1,0:T(8,128)(2,1)S(1)}, u32[]{:S(2)}, u32[]{:S(2)}) collective-permute-start(bf16[128,512]{1,0:T(8,128)(2,1)S(1)} %add_convert_fusion.67), channel_id=1, source_target_pairs={{0,24},{1,25},{2,26},{3,27},{4,28},{5,29},{6,30},{7,31},{8,0},{9,1... | collective-permute-start | bytes 393224 | tf_op jit(solution)/shard_map/ppermute | solution.py:78
  380.1 14.1 %collective-permute-start.40 = (bf16[128,512]{1,0:T(8,128)(2,1)S(1)}, bf16[128,512]{1,0:T(8,128)(2,1)S(1)}, u32[]{:S(2)}, u32[]{:S(2)}) collective-permute-start(bf16[128,512]{1,0:T(8,128)(2,1)S(1)} %add_convert_fusion.67), channel_id=1, source_target_pairs={{0,8},{1,9},{2,10},{3,11},{4,12},{5,13},{6,14},{7,15},{8,16},{9,17... | collective-permute-start | bytes 393224 | tf_op jit(solution)/shard_map/ppermute | solution.py:79
  416.3 14.4 %collective-permute-start.43 = (bf16[128,512]{1,0:T(8,128)(2,1)S(1)}, bf16[128,512]{1,0:T(8,128)(2,1)S(1)}, u32[]{:S(2)}, u32[]{:S(2)}) collective-permute-start(bf16[128,512]{1,0:T(8,128)(2,1)S(1)} %add_convert_fusion.66), channel_id=1, source_target_pairs={{0,24},{1,25},{2,26},{3,27},{4,28},{5,29},{6,30},{7,31},{8,0},{9,1... | collective-permute-start | bytes 393224 | tf_op jit(solution)/shard_map/ppermute | solution.py:78
  453.2 14.4 %collective-permute-start.47 = (bf16[128,512]{1,0:T(8,128)(2,1)S(1)}, bf16[128,512]{1,0:T(8,128)(2,1)S(1)}, u32[]{:S(2)}, u32[]{:S(2)}) collective-permute-start(bf16[128,512]{1,0:T(8,128)(2,1)S(1)} %add_convert_fusion.65), channel_id=1, source_target_pairs={{0,24},{1,25},{2,26},{3,27},{4,28},{5,29},{6,30},{7,31},{8,0},{9,1... | collective-permute-start | bytes 393224 | tf_op jit(solution)/shard_map/ppermute | solution.py:78
  490.2 14.8 %collective-permute-start.51 = (bf16[128,512]{1,0:T(8,128)(2,1)S(1)}, bf16[128,512]{1,0:T(8,128)(2,1)S(1)}, u32[]{:S(2)}, u32[]{:S(2)}) collective-permute-start(bf16[128,512]{1,0:T(8,128)(2,1)S(1)} %add_convert_fusion.64), channel_id=1, source_target_pairs={{0,24},{1,25},{2,26},{3,27},{4,28},{5,29},{6,30},{7,31},{8,0},{9,1... | collective-permute-start | bytes 393224 | tf_op jit(solution)/shard_map/ppermute | solution.py:78
  491.4 14.3 %collective-permute-start.52 = (bf16[128,512]{1,0:T(8,128)(2,1)S(1)}, bf16[128,512]{1,0:T(8,128)(2,1)S(1)}, u32[]{:S(2)}, u32[]{:S(2)}) collective-permute-start(bf16[128,512]{1,0:T(8,128)(2,1)S(1)} %add_convert_fusion.64), channel_id=1, source_target_pairs={{0,8},{1,9},{2,10},{3,11},{4,12},{5,13},{6,14},{7,15},{8,16},{9,17... | collective-permute-start | bytes 393224 | tf_op jit(solution)/shard_map/ppermute | solution.py:79
  527.6 14.4 %collective-permute-start.55 = (bf16[128,512]{1,0:T(8,128)(2,1)S(1)}, bf16[128,512]{1,0:T(8,128)(2,1)S(1)}, u32[]{:S(2)}, u32[]{:S(2)}) collective-permute-start(bf16[128,512]{1,0:T(8,128)(2,1)S(1)} %add_convert_fusion.63), channel_id=1, source_target_pairs={{0,24},{1,25},{2,26},{3,27},{4,28},{5,29},{6,30},{7,31},{8,0},{9,1... | collective-permute-start | bytes 393224 | tf_op jit(solution)/shard_map/ppermute | solution.py:78
  564.7 14.4 %collective-permute-start.59 = (bf16[128,512]{1,0:T(8,128)(2,1)S(1)}, bf16[128,512]{1,0:T(8,128)(2,1)S(1)}, u32[]{:S(2)}, u32[]{:S(2)}) collective-permute-start(bf16[128,512]{1,0:T(8,128)(2,1)S(1)} %add_convert_fusion.62), channel_id=1, source_target_pairs={{0,24},{1,25},{2,26},{3,27},{4,28},{5,29},{6,30},{7,31},{8,0},{9,1... | collective-permute-start | bytes 393224 | tf_op jit(solution)/shard_map/ppermute | solution.py:78
  601.6 14.5 %collective-permute-start.63 = (bf16[128,512]{1,0:T(8,128)(2,1)S(1)}, bf16[128,512]{1,0:T(8,128)(2,1)S(1)}, u32[]{:S(2)}, u32[]{:S(2)}) collective-permute-start(bf16[128,512]{1,0:T(8,128)(2,1)S(1)} %add_convert_fusion.61), channel_id=1, source_target_pairs={{0,24},{1,25},{2,26},{3,27},{4,28},{5,29},{6,30},{7,31},{8,0},{9,1... | collective-permute-start | bytes 393224 | tf_op jit(solution)/shard_map/ppermute | solution.py:78
  602.8 14.1 %collective-permute-start.64 = (bf16[128,512]{1,0:T(8,128)(2,1)S(1)}, bf16[128,512]{1,0:T(8,128)(2,1)S(1)}, u32[]{:S(2)}, u32[]{:S(2)}) collective-permute-start(bf16[128,512]{1,0:T(8,128)(2,1)S(1)} %add_convert_fusion.61), channel_id=1, source_target_pairs={{0,8},{1,9},{2,10},{3,11},{4,12},{5,13},{6,14},{7,15},{8,16},{9,17... | collective-permute-start | bytes 393224 | tf_op jit(solution)/shard_map/ppermute | solution.py:79
  692.9 14.7 %collective-permute-start.69 = (bf16[128,512]{1,0:T(8,128)(2,1)S(1)}, bf16[128,512]{1,0:T(8,128)(2,1)S(1)}, u32[]{:S(2)}, u32[]{:S(2)}) collective-permute-start(bf16[128,512]{1,0:T(8,128)(2,1)S(1)} %fusion.911), channel_id=1, source_target_pairs={{0,24},{1,25},{2,26},{3,27},{4,28},{5,29},{6,30},{7,31},{8,0},{9,1... | collective-permute-start | bytes 393224 | tf_op jit(solution)/shard_map/ppermute | solution.py:78
  693.1 14.6 %collective-permute-start.70 = (bf16[128,512]{1,0:T(8,128)(2,1)S(1)}, bf16[128,512]{1,0:T(8,128)(2,1)S(1)}, u32[]{:S(2)}, u32[]{:S(2)}) collective-permute-start(bf16[128,512]{1,0:T(8,128)(2,1)S(1)} %fusion.911), channel_id=1, source_target_pairs={{0,8},{1,9},{2,10},{3,11},{4,12},{5,13},{6,14},{7,15},{8,16},{9,17... | collective-permute-start | bytes 393224 | tf_op jit(solution)/shard_map/ppermute | solution.py:79
  770.8 14.1 %collective-permute-start.81 = (bf16[128,512]{1,0:T(8,128)(2,1)S(1)}, bf16[128,512]{1,0:T(8,128)(2,1)S(1)}, u32[]{:S(2)}, u32[]{:S(2)}) collective-permute-start(bf16[128,512]{1,0:T(8,128)(2,1)S(1)} %add_convert_fusion.57), channel_id=1, source_target_pairs={{0,24},{1,25},{2,26},{3,27},{4,28},{5,29},{6,30},{7,31},{8,0},{9,1... | collective-permute-start | bytes 393224 | tf_op jit(solution)/shard_map/ppermute | solution.py:78
  938.0 14.0 %collective-permute-start.105 = (bf16[128,512]{1,0:T(8,128)(2,1)S(1)}, bf16[128,512]{1,0:T(8,128)(2,1)S(1)}, u32[]{:S(2)}, u32[]{:S(2)}) collective-permute-start(bf16[128,512]{1,0:T(8,128)(2,1)S(1)} %add_convert_fusion.51), channel_id=1, source_target_pairs={{0,24},{1,25},{2,26},{3,27},{4,28},{5,29},{6,30},{7,31},{8,0},{9,1... | collective-permute-start | bytes 393224 | tf_op jit(solution)/shard_map/ppermute | solution.py:78
  1021.6 14.0 %collective-permute-start.117 = (bf16[128,512]{1,0:T(8,128)(2,1)S(1)}, bf16[128,512]{1,0:T(8,128)(2,1)S(1)}, u32[]{:S(2)}, u32[]{:S(2)}) collective-permute-start(bf16[128,512]{1,0:T(8,128)(2,1)S(1)} %add_convert_fusion.48), channel_id=1, source_target_pairs={{0,24},{1,25},{2,26},{3,27},{4,28},{5,29},{6,30},{7,31},{8,0},{9,1... | collective-permute-start | bytes 393224 | tf_op jit(solution)/shard_map/ppermute | solution.py:78
  1105.1 14.0 %collective-permute-start.129 = (bf16[128,512]{1,0:T(8,128)(2,1)S(1)}, bf16[128,512]{1,0:T(8,128)(2,1)S(1)}, u32[]{:S(2)}, u32[]{:S(2)}) collective-permute-start(bf16[128,512]{1,0:T(8,128)(2,1)S(1)} %add_convert_fusion.45), channel_id=1, source_target_pairs={{0,24},{1,25},{2,26},{3,27},{4,28},{5,29},{6,30},{7,31},{8,0},{9,1... | collective-permute-start | bytes 393224 | tf_op jit(solution)/shard_map/ppermute | solution.py:78
  (208 other events, 2315.8 us)
where the time goes:
time: 1170 us; the launch traced here: 1150 us
  matrix products  427 us (36%)
  starting transfers between devices  284 us (24%)
  local copies, waits for them, and re-layouts  252 us (22%)
  other arithmetic  178 us (15%)
    dot_general x186, matrix products, matmul_f32(): return jnp.dot(values, weight, preferred_element_type=jnp.float32)  425 us
    ppermute x32, starting transfers between devices, local_run(): next_head = lax.ppermute(mesh_cur[:half_shard], 'gp', shift_pairs(-1))  210 us
    unnamed x489, local copies, waits for them, and re-layouts  194 us
    reduce_sum x80, other arithmetic, layer_norm(): spread = jnp.mean(centred * centred, axis=-1, keepdims=True)  69.5 us
    reduce_sum x32, other arithmetic, local_run(): edge_sum = jnp.sum(edge_lat, axis=1, dtype=jnp.float32).astype(jnp.bfloat16)  64.2 us
    ppermute x32, starting transfers between devices, local_run(): far_plus = lax.ppermute(mesh_cur, 'gp', shift_pairs(-quarter_hop))  44.4 us
    convert_element_type x38, other arithmetic, residual(): return (base.astype(jnp.float32) + update).astype(jnp.bfloat16)  27.5 us
  transfers between devices with their start and end apart: 132, of which 4 were waited for; matrix products, arithmetic and copies ran while one was open for 20% of the time, Pallas kernels for 0%

commit v1 on v0

v1 whole, which is shorter than its diff:
```python
import functools
import math

import jax
import jax.numpy as jnp
from jax import lax
from jax.experimental import pallas as pl
from jax.experimental.pallas import tpu as pltpu
from jax.sharding import PartitionSpec as P

F32 = jnp.float32
BF16 = jnp.bfloat16
LANES = 128
QUARTERS = 4
EDGE_KINDS = 6


def chip_ring(side):
    order = list(range(side))
    for y in range(1, side):
        columns = range(1, side)
        order += [y * side + x for x in (reversed(columns) if y % 2 else columns)]
    order += [y * side for y in range(side - 1, 0, -1)]
    return order


def dot(left, right):
    return jnp.dot(left, right, preferred_element_type=F32)


def silu(values):
    half = 0.5 * values
    return half + half * jnp.tanh(half)


def layer_norm(values):
    centred = values - jnp.mean(values, axis=-1, keepdims=True)
    spread = jnp.mean(centred * centred, axis=-1, keepdims=True)
    return centred * lax.rsqrt(spread + 1e-5)


def tail(pre_act, w_second):
    return layer_norm(dot(silu(pre_act).astype(BF16), w_second))


def pick(index, table):
    found = jnp.int32(0)
    for position, value in enumerate(table):
        found = found + jnp.where(index == position, jnp.int32(value), jnp.int32(0))
    return found


def rows_mod(shape, modulus):
    return lax.broadcasted_iota(jnp.int32, shape, 0) & (modulus - 1)


def next_quarter(values):
    rows = values.shape[0]
    return jnp.where(rows_mod(values.shape, 4) < 3, pltpu.roll(values, rows - 1, 0), pltpu.roll(values, 3, 0))


def prev_quarter(values):
    rows = values.shape[0]
    return jnp.where(rows_mod(values.shape, 4) > 0, pltpu.roll(values, 1, 0), pltpu.roll(values, rows - 3, 0))


def kernel(cfg, xp_in, xc_in, gf_in, mf_in, ns_in, wpad, wfin, wembed_h, win_h, wout_h, nin_h, nout_h, wself_h, whid_h,
           out_a, out_b,
           wembed, win, wout, nin, nout, wself, whid, state, perm, mf_next, mf_all, mf_blk,
           fst_s, fst_r, stage_s, stage_r, back_s, back_r,
           mesh_buf, edge_a, edge_b, halo_b, halo_c,
           edges, edge_base, mesh_lat, g2m_lat, m2g_lat, grid_lat, grid_cur,
           enc_base, enc_node, dec_base, dec_static, dec_node, mesh_band,
           proj, recv, node_pre, acc, tail_pre, beside, far,
           misc_sem, wl_sem, shift_sem, fst_ss, fst_rs, stg_ss, stg_rs, bck_ss, bck_rs, halo_ss, halo_rs):
    group, ring, latent, ratio, layers, half = cfg
    chips = len(ring)
    mesh_dev = chips * 8
    step_rows = mesh_dev // QUARTERS
    me = lax.axis_index("gp")
    core = me % 2
    where_of = [0] * chips
    for position, chip in enumerate(ring):
        where_of[chip] = position
    place = pick(me // 2, where_of)
    chip_up = pick(place, ring[1:] + ring[:1])
    chip_down = pick(place, ring[-1:] + ring[:-1])
    is_last = place == chips - 1
    is_first = place == 0
    band_core = (me % 8) // 4
    band_slot = (me // 8) * 4 + me % 4
    other = me + 1 - 2 * core

    def target(index):
        return dict(device_id={"gp": index}, device_id_type=pl.DeviceIdType.MESH)

    def local(source, dest, sem):
        return pltpu.make_async_copy(source, dest, sem)

    def block_copies(block, slot):
        return [local(win_h.at[block], win.at[slot], wl_sem.at[slot, 0]), local(wout_h.at[block], wout.at[slot], wl_sem.at[slot, 1]),
                local(nin_h.at[block], nin.at[slot], wl_sem.at[slot, 2]), local(nout_h.at[block], nout.at[slot], wl_sem.at[slot, 3])]

    embed_copy = local(wembed_h, wembed, misc_sem.at[0])
    self_copy = local(wself_h, wself, misc_sem.at[1])
    hid_copy = local(whid_h, whid, misc_sem.at[2])
    enc_copies = block_copies(0, 2)
    dec_copies = block_copies(layers + 1, 3)
    for copy in [embed_copy] + enc_copies + [self_copy] + dec_copies + [hid_copy] + block_copies(1, 0):
        copy.start()

    barrier = pltpu.get_barrier_semaphore()
    for hop in range(1, group):
        pl.semaphore_signal(barrier, inc=1, **target(lax.rem(me + hop, group)))

    row = lax.broadcasted_iota(jnp.int32, (mesh_dev, mesh_dev), 0)
    col = lax.broadcasted_iota(jnp.int32, (mesh_dev, mesh_dev), 1)

    def by_chip(index):
        return ((index >> 2) & 1) * half + (index >> 3) * 4 + (index & 3)

    def by_source(index):
        b = (index >> 2) & 7
        return ((index & 3) * 4 + (b >> 1)) * 8 + (b & 1) * 4 + (index >> 5)

    for slot, mask in enumerate((by_chip(row) == col, by_source(row) == col, row == by_source(col), row == by_chip(col))):
        perm[slot] = jnp.where(mask, 1.0, 0.0).astype(BF16)

    for ref in (halo_c, enc_base, enc_node, dec_base, dec_node, dec_static, acc, proj, recv, node_pre, tail_pre, beside, far):
        ref[...] = jnp.zeros_like(ref)
    state[...] = jnp.zeros_like(state)
    for r in range(ratio):
        state[0, r, :, :xp_in.shape[1]] = xp_in[pl.ds(r, mesh_dev, stride=ratio), :]
        state[1, r, :, :xc_in.shape[1]] = xc_in[pl.ds(r, mesh_dev, stride=ratio), :]

    pl.semaphore_wait(barrier, group - 1)
    shift = pltpu.make_async_remote_copy(mf_in.at[pl.ds(0, half)], mf_next, shift_sem.at[0], shift_sem.at[1],
                                         **target(lax.rem(me + group - 1, group)))
    shift.start()

    def exchange(src, dst, send_sem, recv_sem, slot, dest_of, source_of):
        copies = []
        for part in range(chips):
            dest = dest_of(part)
            copy = pltpu.make_async_remote_copy(src.at[part], dst.at[slot], send_sem.at[part], recv_sem.at[slot], **target(dest))
            copies.append((dest, copy))

            @pl.when(dest != me)
            def _(copy=copy):
                copy.start()

            @pl.when(dest == me)
            def _(part=part):
                dst[slot] = src[part]

        def finish():
            for part in range(chips):
                origin = source_of(part)

                @pl.when(origin != me)
                def _(part=part):
                    pltpu.make_async_remote_copy(src.at[part], dst.at[part], send_sem.at[part], recv_sem.at[part], **target(other)).wait_recv()

            for dest, copy in copies:
                @pl.when(dest != me)
                def _(copy=copy):
                    copy.wait_send()
        return finish

    def forth(src, dst, send_sem, recv_sem):
        return exchange(src, dst, send_sem, recv_sem, band_slot, lambda p: 2 * ring[p] + band_core,
                        lambda q: (q // 4) * 8 + core * 4 + q % 4)

    def back(src, dst, send_sem, recv_sem):
        return exchange(src, dst, send_sem, recv_sem, place, lambda q: (q // 4) * 8 + core * 4 + q % 4,
                        lambda p: 2 * ring[p] + band_core)

    embed_copy.wait()
    for r in range(ratio):
        m2g_lat[r] = tail(dot(gf_in[r], wpad[4]), wembed[3]).astype(BF16)
    shift.wait()
    mf_all[:half] = mf_in[half:]
    mf_all[half:] = mf_next[...]
    feats = mf_all[...]
    fst_s[...] = dot(perm[0], feats).astype(BF16).reshape(fst_s.shape)
    fst_done = forth(fst_s, fst_r, fst_ss, fst_rs)
    mesh_lat[...] = tail(dot(feats, wpad[5 + EDGE_KINDS]), wembed[1]).astype(BF16)
    for copy in enc_copies:
        copy.wait()
    recv[...] = dot(mesh_lat[...], win[2, 2 * latent:])
    enc_node[...] = dot(mesh_lat[...], nin[2, :latent])
    for r in range(ratio):
        g2m_lat[r] = tail(dot(feats, wpad[6 + EDGE_KINDS + r]), wembed[2]).astype(BF16)
        enc_base[r] = recv[...] + dot(g2m_lat[r], win[2, :latent])
    for copy in dec_copies:
        copy.wait()
    for r in range(ratio):
        dec_static[r] = dot(m2g_lat[r], win[3, :latent])
    fst_done()
    mf_blk[...] = dot(perm[1], fst_r[...].reshape(mesh_dev, LANES)).astype(BF16)
    for k in range(EDGE_KINDS):
        edge_base[k] = tail(dot(mf_blk[...], wpad[5 + k]), wembed[4]).astype(BF16)
    self_copy.wait()
    hid_copy.wait()

    low = lax.broadcasted_iota(jnp.int32, (8, latent), 0) < 4

    def put_mesh(slot, values):
        mesh_buf[slot] = values.astype(BF16)
        heads = [values[c * step_rows:c * step_rows + 8] for c in range(4)]
        tails = [values[(c + 1) * step_rows - 8:(c + 1) * step_rows] for c in range(4)]
        edge_a[slot] = jnp.concatenate([jnp.where(low, heads[0], pltpu.roll(heads[1], 4, 0)),
                                        jnp.where(low, heads[2], pltpu.roll(heads[3], 4, 0))], axis=0).astype(BF16)
        edge_b[slot] = jnp.concatenate([jnp.where(low, pltpu.roll(tails[0], 4, 0), tails[1]),
                                        jnp.where(low, pltpu.roll(tails[2], 4, 0), tails[3])], axis=0).astype(BF16)

    def halo_copies(slot):
        def send(src, dst, kind, dest):
            return pltpu.make_async_remote_copy(src, dst, halo_ss.at[slot, kind], halo_rs.at[slot, kind], **target(dest))
        near = [send(mesh_buf.at[slot, pl.ds(0, step_rows)], halo_c.at[slot, pl.ds(0, step_rows)], 0, 2 * chip_down + core),
                send(mesh_buf.at[slot, pl.ds(mesh_dev - step_rows, step_rows)], halo_c.at[slot, pl.ds(step_rows, step_rows)], 1, 2 * chip_up + core)]
        pair = [send(edge_a.at[slot], halo_b.at[slot, pl.ds(0, 16)], 2, other),
                send(edge_b.at[slot], halo_b.at[slot, pl.ds(16, 16)], 3, other)]
        seam_a = send(edge_a.at[slot], halo_c.at[slot, pl.ds(2 * step_rows, 16)], 4, 2 * chip_down + 1 - core)
        seam_b = send(edge_b.at[slot], halo_c.at[slot, pl.ds(2 * step_rows + 16, 16)], 5, 2 * chip_up + 1 - core)
        return near, pair, seam_a, seam_b

    def run_layer(step, layer):
        slot = layer % 2
        later = 1 - slot
        near, pair, seam_a, seam_b = halo_copies(slot)
        near[0].start()
        near[1].start()

        @pl.when(is_first)
        def _():
            seam_a.start()

        @pl.when(is_last)
        def _():
            seam_b.start()
        pair[0].start()
        pair[1].start()

        for copy in block_copies(layer + 1, slot):
            copy.wait()

        @pl.when(jnp.logical_or(step == 0, layer < layers - 1))
        def _():
            for copy in block_copies(1 + (layer + 1) % layers, later):
                copy.start()

        w_edge = win.at[slot]
        w_edge_two = wout.at[slot]
        w_node = nin.at[slot]
        w_node_two = nout.at[slot]

        @pl.when(layer == 0)
        def _():
            edges[...] = edge_base[...]

        nodes = mesh_buf[slot]
        proj[...] = dot(nodes, w_edge[latent:2 * latent])
        recv[...] = dot(nodes, w_edge[2 * latent:])

        def edge_part(kind, lo, hi, sent, first=False):
            old = edges[kind, lo:hi]
            pre = dot(old, w_edge[:latent]) + sent + recv[lo:hi]
            new = (old.astype(F32) + tail(pre, w_edge_two[...])).astype(BF16)
            edges[kind, lo:hi] = new
            if first:
                acc[lo:hi] = new.astype(F32)
            else:
                acc[lo:hi] = acc[lo:hi] + new.astype(F32)

        edge_part(4, 0, mesh_dev, next_quarter(proj[...]), first=True)
        edge_part(5, 0, mesh_dev, prev_quarter(proj[...]))
        edge_part(0, 0, mesh_dev - step_rows, proj[step_rows:])
        edge_part(1, step_rows, mesh_dev, proj[:mesh_dev - step_rows])
        node_pre[...] = dot(nodes, w_node[:latent])
        tail_pre[:step_rows] = dot(edges[0, mesh_dev - step_rows:], w_edge[:latent]) + recv[mesh_dev - step_rows:]
        tail_pre[step_rows:] = dot(edges[1, :step_rows], w_edge[:latent]) + recv[:step_rows]

        pair[0].wait_recv()
        pair[1].wait_recv()
        beside[...] = dot(halo_b[slot], w_edge[latent:2 * latent])
        above = jnp.where(core == 1, next_quarter(beside[:16]), beside[:16])
        below = jnp.where(core == 0, prev_quarter(beside[16:]), beside[16:])
        for kind, halo, shifted in ((2, above, pltpu.roll(proj[...], mesh_dev - 4, 0)), (3, below, pltpu.roll(proj[...], 4, 0))):
            parts = []
            for c in range(4):
                piece = halo[(c // 2) * 8:(c // 2) * 8 + 8]
                lo, hi = c * step_rows, (c + 1) * step_rows
                if kind == 2:
                    piece = piece if c % 2 else pltpu.roll(piece, 4, 0)
                    parts += [shifted[lo:hi - 8], jnp.where(low, shifted[hi - 8:hi], piece)]
                else:
                    piece = pltpu.roll(piece, 4, 0) if c % 2 else piece
                    parts += [jnp.where(low, piece, shifted[lo:lo + 8]), shifted[lo + 8:hi]]
            edge_part(kind, 0, mesh_dev, jnp.concatenate(parts, axis=0))

        near[0].wait_recv()
        near[1].wait_recv()

        @pl.when(is_last)
        def _():
            seam_a.wait_recv()

        @pl.when(is_first)
        def _():
            seam_b.wait_recv()
        far[...] = dot(halo_c[slot], w_edge[latent:2 * latent])
        up, down = far[:step_rows], far[step_rows:2 * step_rows]
        up_seam = far[2 * step_rows:2 * step_rows + 8]
        up_seam = pltpu.roll(jnp.where(core == 1, next_quarter(up_seam), up_seam), 4, 0)
        down_seam = far[2 * step_rows + 24:]
        down_seam = pltpu.roll(jnp.where(core == 0, prev_quarter(down_seam), down_seam), 4, 0)
        up_moved = pltpu.roll(up, step_rows - 4, 0)
        up_moved = jnp.concatenate([up_moved[:step_rows - 8], jnp.where(low, up_moved[step_rows - 8:], up_seam)], axis=0)
        down_moved = pltpu.roll(down, 4, 0)
        down_moved = jnp.concatenate([jnp.where(low, down_seam, down_moved[:8]), down_moved[8:]], axis=0)
        sent = jnp.concatenate([jnp.where(is_last, up_moved, up), jnp.where(is_first, down_moved, down)], axis=0)
        update = tail(tail_pre[...] + sent, w_edge_two[...])
        new_up = (edges[0, mesh_dev - step_rows:].astype(F32) + update[:step_rows]).astype(BF16)
        new_down = (edges[1, :step_rows].astype(F32) + update[step_rows:]).astype(BF16)
        edges[0, mesh_dev - step_rows:] = new_up
        edges[1, :step_rows] = new_down
        total = jnp.concatenate([acc[:step_rows] + new_down.astype(F32), acc[step_rows:mesh_dev - step_rows],
                                 acc[mesh_dev - step_rows:] + new_up.astype(F32)], axis=0).astype(BF16)
        update = tail(node_pre[...] + dot(total, w_node[latent:]), w_node_two[...])
        fresh = (nodes.astype(F32) + update).astype(BF16).astype(F32)
        near[0].wait_send()
        near[1].wait_send()
        pair[0].wait_send()
        pair[1].wait_send()

        @pl.when(is_first)
        def _():
            seam_a.wait_send()

        @pl.when(is_last)
        def _():
            seam_b.wait_send()
        put_mesh(later, fresh)

    mean, spread, diff_mean, diff_spread = ns_in[0:1], ns_in[1:2], ns_in[2:3], ns_in[3:4]

    def run_step(step):
        after = lax.rem(step + 2, 3)
        for r in range(ratio):
            past = ((state[step, r] - mean) / spread).astype(BF16)
            now = ((state[step + 1, r] - mean) / spread).astype(BF16)
            pre = dot(past, wpad[0]) + dot(now, wpad[1]) + dot(gf_in[r], wpad[2 + step])
            lat = tail(pre, wembed[0]).astype(BF16)
            grid_lat[r] = lat
            pre = enc_base[r] + dot(lat, win[2, latent:2 * latent])
            new = (g2m_lat[r].astype(F32) + tail(pre, wout[2])).astype(BF16).astype(F32)
            acc[...] = new if r == 0 else acc[...] + new
        update = tail(enc_node[...] + dot(acc[...].astype(BF16), nin[2, latent:]), nout[2])
        encoded = (mesh_lat[...].astype(F32) + update).astype(BF16)
        stage_s[...] = dot(perm[0], encoded).astype(BF16).reshape(stage_s.shape)
        arrive = forth(stage_s, stage_r, stg_ss, stg_rs)
        for r in range(ratio):
            lat = grid_lat[r]
            cur = (lat.astype(F32) + tail(dot(lat, wself[0]), wself[1])).astype(BF16)
            grid_cur[r] = cur
            dec_base[r] = dec_static[r] + dot(cur, win[3, 2 * latent:])
            dec_node[r] = dot(cur, nin[3, :latent])
        arrive()
        acc[...] = dot(perm[1], stage_r[...].reshape(mesh_dev, latent))
        put_mesh(0, acc[...])

        @pl.loop(0, layers)
        def _(layer):
            run_layer(step, layer)

        back_s[...] = dot(perm[2], mesh_buf[layers % 2]).astype(BF16).reshape(back_s.shape)
        back(back_s, back_r, bck_ss, bck_rs)()
        mesh_band[...] = dot(perm[3], back_r[...].reshape(mesh_dev, latent)).astype(BF16)
        recv[...] = dot(mesh_band[...], win[3, latent:2 * latent])
        for r in range(ratio):
            dec_edge = (m2g_lat[r].astype(F32) + tail(dec_base[r] + recv[...], wout[3])).astype(BF16)
            update = tail(dec_node[r] + dot(dec_edge, nin[3, latent:]), nout[3])
            grid_out = (grid_cur[r].astype(F32) + update).astype(BF16)
            hidden = silu(dot(grid_out, whid[...])).astype(BF16)
            fresh = state[step + 1, r] + diff_spread * dot(hidden, wfin[...]) + diff_mean
            state[after, r] = fresh

            @pl.when(step == 0)
            def _():
                out_a[pl.ds(r, mesh_dev, stride=ratio), :] = fresh[:, :out_a.shape[1]]

            @pl.when(step == 1)
            def _():
                out_b[pl.ds(r, mesh_dev, stride=ratio), :] = fresh[:, :out_b.shape[1]]

    @pl.loop(0, 2)
    def _(step):
        run_step(step)


def solution(mesh):
    group = mesh.shape["gp"]
    side = math.isqrt(group // 2)
    ring = chip_ring(side)
    row_spec = P(("dp", "gp"))
    edge_spec = P(("dp", "gp"), None, None)
    whole = P()

    def local_run(x_prev, x_cur, forcing, grid_static, g2m_feat, m2g_feat, mesh_feat, mesh_edge_feat, norm_stats, w_grid_in, w_mesh_in, w_eemb_in, w_embed_out, w_edge_in, w_edge_out, w_node_in, w_node_out, w_grid_self, w_out_hidden, w_out_final):
        grid_dev, variables = x_prev.shape
        mesh_dev = mesh_feat.shape[0]
        ratio = grid_dev // mesh_dev
        latent = w_embed_out.shape[-1]
        layers = w_edge_in.shape[0] - 2
        steps, force = forcing.shape[1:]
        fixed = grid_static.shape[1]
        efeat = m2g_feat.shape[1]
        assert side * side * 2 == group and mesh_dev == 8 * len(ring) and mesh_dev == 128 and ratio == 4 and layers % 2 == 0

        def lanes(values, fill=0):
            return jnp.pad(values, [(0, 0)] * (values.ndim - 1) + [(0, LANES - values.shape[-1])], constant_values=fill)

        gf = jnp.concatenate([forcing.reshape(grid_dev, steps * force), grid_static, m2g_feat], axis=1).astype(BF16)
        gf = lanes(gf.reshape(mesh_dev, ratio, gf.shape[1]).transpose(1, 0, 2))
        kinds = mesh_edge_feat.shape[1]
        mf = lanes(jnp.concatenate([mesh_edge_feat.reshape(mesh_dev, kinds * efeat), mesh_feat,
                                    g2m_feat.reshape(mesh_dev, ratio * efeat)], axis=1).astype(BF16))
        ns = jnp.stack([lanes(norm_stats[0]), lanes(norm_stats[1], 1), lanes(norm_stats[2]), lanes(norm_stats[3])])

        def placed(*pieces):
            total = 0
            for start, rows in pieces:
                total = total + jnp.pad(rows, ((start, LANES - start - rows.shape[0]), (0, 0)))
            return total

        w_force = w_grid_in[2 * variables:2 * variables + force]
        w_fixed = w_grid_in[2 * variables + force:]
        start = steps * force
        pads = [placed((0, w_grid_in[:variables])), placed((0, w_grid_in[variables:2 * variables])),
                placed((0, w_force), (start, w_fixed)), placed((force, w_force), (start, w_fixed)),
                placed((start + fixed, w_eemb_in[1]))]
        pads += [placed((k * efeat, w_eemb_in[2])) for k in range(kinds)]
        pads += [placed((kinds * efeat, w_mesh_in))]
        pads += [placed((kinds * efeat + mesh_feat.shape[1] + r * efeat, w_eemb_in[0])) for r in range(ratio)]
        wpad = jnp.stack(pads)
        wfin = lanes(w_out_final)

        vmem = pl.BlockSpec(memory_space=pltpu.VMEM)
        hbm = pl.BlockSpec(memory_space=pl.ANY)
        chips = len(ring)
        step_rows = mesh_dev // QUARTERS
        VM = pltpu.VMEM
        DMA = pltpu.SemaphoreType.DMA
        grid_shape = (ratio, mesh_dev, latent)
        scratch = [
            VM(w_embed_out.shape, BF16), VM((4,) + w_edge_in.shape[1:], BF16), VM((4,) + w_edge_out.shape[1:], BF16),
            VM((4,) + w_node_in.shape[1:], BF16), VM((4,) + w_node_out.shape[1:], BF16), VM(w_grid_self.shape, BF16), VM(w_out_hidden.shape, BF16),
            VM((3, ratio, mesh_dev, LANES), F32), VM((4, mesh_dev, mesh_dev), BF16),
            VM((mesh_dev // 2, LANES), BF16), VM((mesh_dev, LANES), BF16), VM((mesh_dev, LANES), BF16),
            VM((chips, 8, LANES), BF16), VM((chips, 8, LANES), BF16),
            VM((chips, 8, latent), BF16), VM((chips, 8, latent), BF16), VM((chips, 8, latent), BF16), VM((chips, 8, latent), BF16),
            VM((2, mesh_dev, latent), BF16), VM((2, 16, latent), BF16), VM((2, 16, latent), BF16), VM((2, 32, latent), BF16), VM((2, 2 * step_rows + 32, latent), BF16),
            VM((EDGE_KINDS, mesh_dev, latent), BF16), VM((EDGE_KINDS, mesh_dev, latent), BF16), VM((mesh_dev, latent), BF16),
            VM(grid_shape, BF16), VM(grid_shape, BF16), VM(grid_shape, BF16), VM(grid_shape, BF16),
            VM(grid_shape, F32), VM((mesh_dev, latent), F32), VM(grid_shape, F32), VM(grid_shape, F32), VM(grid_shape, F32), VM((mesh_dev, latent), BF16),
            VM((mesh_dev, latent), F32), VM((mesh_dev, latent), F32), VM((mesh_dev, latent), F32), VM((mesh_dev, latent), F32), VM((2 * step_rows, latent), F32), VM((32, latent), F32), VM((2 * step_rows + 32, latent), F32),
            DMA((3,)), DMA((4, 4)), DMA((2,)), DMA((chips,)), DMA((chips,)), DMA((chips,)), DMA((chips,)), DMA((chips,)), DMA((chips,)), DMA((2, 6)), DMA((2, 6)),
        ]
        cfg = (group, ring, latent, ratio, layers, mesh_dev // 2)
        return pl.pallas_call(
            functools.partial(kernel, cfg),
            out_shape=(jax.ShapeDtypeStruct(x_cur.shape, F32),) * 2,
            in_specs=[vmem] * 7 + [hbm] * 7,
            out_specs=(vmem, vmem),
            scratch_shapes=scratch,
            compiler_params=pltpu.CompilerParams(collective_id=0, has_side_effects=True, vmem_limit_bytes=60 * 1024 * 1024),
        )(x_prev, x_cur, gf, mf, ns, wpad, wfin, w_embed_out, w_edge_in, w_edge_out, w_node_in, w_node_out, w_grid_self, w_out_hidden)

    in_specs = (row_spec, row_spec, edge_spec, row_spec, row_spec, row_spec, row_spec, edge_spec, whole) + (whole,) * 11
    return jax.shard_map(local_run, mesh=mesh, in_specs=in_specs, out_specs=(row_spec, row_spec), check_vma=False)
```

time: 1170 us -> 213 us (0.18); the launches traced: 1150 us -> 213 us
  matrix products: 427 us -> 0 us
  starting transfers between devices: 284 us -> 0 us
  local copies, waits for them, and re-layouts: 252 us -> 15.1 us
  Pallas kernels: 0 us -> 194 us
  other arithmetic: 178 us -> 2.51 us
    dot_general x187 -> x0, matrix products: 427 us -> none  [the longest x186 425 us: matmul_f32(): return jnp.dot(values, weight, preferred_element_type=jnp.float32)]
    ppermute x132 -> x0, starting transfers between devices: 284 us -> none  [the longest x32 210 us: local_run(): next_head = lax.ppermute(mesh_cur[:half_shard], 'gp', shift_pairs(-1))]
    pallas_call x0 -> x1, Pallas kernels: none -> 194 us  [local_run(): pl.pallas_call(functools.partial(kernel, cfg), out_shape=(jax.ShapeDtypeS...]
    unnamed x489 -> x37, local copies, waits for them, and re-layouts: 194 us -> 2.76 us
    reduce_sum x114 -> x0, other arithmetic: 136 us -> none  [the longest x80 69.5 us: layer_norm(): spread = jnp.mean(centred * centred, axis=-1, keepdims=True)]
    convert_element_type x41 -> x0, other arithmetic: 27.9 us -> none  [the longest x38 27.5 us: residual(): return (base.astype(jnp.float32) + update).astype(jnp.bfloat16)]
    another operation x32 -> x6, local copies, waits for them, and re-layouts: 21.8 us -> 0.34 us  [local_run(): jnp.stack([send_proj[half_shard + 1:half_shard + 1 + mesh_dev], send_proj...]
    concatenate x32 -> x6, local copies, waits for them, and re-layouts: 20.1 us -> 4.45 us  [local_run(): jnp.concatenate([forcing.reshape(grid_dev, steps * force), grid_static, m...]
  transfers between devices with their start and end apart: 132 -> 0, of which waited for: 4 -> 0; matrix products, arithmetic and copies ran while one was open for 20% -> 0% of each run, Pallas kernels for 0% -> 0%
where the time goes in v1:
time: 213 us
  Pallas kernels  194 us (91%)
  local copies, waits for them, and re-layouts  15.1 us (7%)
  other arithmetic  2.51 us (1%)
    pallas_call x1, Pallas kernels, local_run(): pl.pallas_call(functools.partial(kernel, cfg), out_shape=(jax.ShapeDtypeS...  194 us
    concatenate x6, local copies, waits for them, and re-layouts, local_run(): jnp.concatenate([forcing.reshape(grid_dev, steps * force), grid_static, m...  4.45 us

profile of v1, /device:TPU:97, one launch (start us, length us, event | category | flops | bytes accessed | tf_op | source)
XLA Modules:
  0.0 213.0 jit_solution(13417911938430356678)
XLA Ops:
  0.7 0.8 fusion.9
  1.5 1.0 bitcast_dynamic-update-slice_fusion.13
  2.5 0.9 slice.47
  3.4 0.7 slice_bitcast_fusion
  4.4 0.7 bitcast_dynamic-update-slice_fusion.4
  5.2 0.6 pad_maximum_fusion.ns_in
  5.9 0.7 concatenate.15
  6.6 1.0 copy.56
  7.6 0.4 concatenate.16
  8.0 1.0 copy.57
  9.1 0.3 concatenate.17
  9.4 1.0 copy.58
  10.4 0.2 maximum_bitcast_fusion
  10.6 0.7 pad.93.gf_in
  11.3 0.2 copy.59
  11.7 0.1 copy.61
  11.9 0.7 fusion.8.mf_in
  12.6 0.9 copy.63.xp_in
  13.4 0.9 copy.64.xc_in
  14.3 0.1 copy.62
  14.4 0.7 pad.116.wfin
  15.1 194.3 %shard_map.203 = (f32[512,83]{1,0:T(8,128)}, f32[512,83]{1,0:T(8,128)}) custom-call(f32[512,83]{1,0:T(8,128)} %copy.63.xp_in, f32[512,83]{1,0:T(8,128)} %copy.64.xc_in, bf16[4,128,128]{2,1,0:T(8,128)(2,1)} %pad.93.gf_in, bf16[128,128]{1,0:T(8,128)(2,1)} %fusion.8.mf_in, f32[4,128]{1,0:T(4,128)} %pad_maximum_fusion.ns_in, bf16[16,128,512]{2,1,0:T(8,128)(2,1)} %copy-done, ...), custom_call_target="tpu_custom_call" | custom-call | tf_op jit(solution)/shard_map/pallas_call | solution.py:471
  209.5 1.8 copy.65
  211.2 1.8 copy.66
  (48 shorter events, 0.5 us)
Async XLA Ops:
  0.6 4.6 %copy-start.10 = (f32[4,83]{1,0:T(4,128)S(1)}, f32[4,83]{1,0:T(4,128)}, u32[]{:S(2)}) copy-start(f32[4,83]{1,0:T(4,128)} %param.28) | copy-start | bytes 3988
  0.6 5.2 %copy-start.4 = (f32[512,2,5]{0,1,2:T(2,128)S(1)}, f32[512,2,5]{0,1,2:T(2,128)}, u32[]{:S(2)}) copy-start(f32[512,2,5]{0,1,2:T(2,128)} %param.22) | copy-start | bytes 61444
  0.7 7.0 %copy-start.5 = (f32[512,5]{0,1:T(8,128)S(1)}, f32[512,5]{0,1:T(8,128)}, u32[]{:S(2)}) copy-start(f32[512,5]{0,1:T(8,128)} %param.23) | copy-start | bytes 30724
  0.7 8.4 %copy-start.7 = (f32[512,4]{0,1:T(4,128)S(1)}, f32[512,4]{0,1:T(4,128)}, u32[]{:S(2)}) copy-start(f32[512,4]{0,1:T(4,128)} %param.25) | copy-start | bytes 24580
  4.2 7.1 %copy-start.8 = (f32[512,4]{0,1:T(4,128)S(1)}, f32[512,4]{0,1:T(4,128)}, u32[]{:S(2)}) copy-start(f32[512,4]{0,1:T(4,128)} %param.24) | copy-start | bytes 24580
  4.2 7.4 %copy-start.6 = (f32[128,6,4]{0,2,1:T(4,128)S(1)}, f32[128,6,4]{0,2,1:T(4,128)}, u32[]{:S(2)}) copy-start(f32[128,6,4]{0,2,1:T(4,128)} %param.27) | copy-start | bytes 36868
  4.2 7.5 %copy-start.9 = (f32[128,3]{0,1:T(4,128)S(1)}, f32[128,3]{0,1:T(4,128)}, u32[]{:S(2)}) copy-start(f32[128,3]{0,1:T(4,128)} %param.26) | copy-start | bytes 4612
  4.3 8.3 %copy-start.1 = (f32[512,83]{0,1:T(8,128)S(1)}, f32[512,83]{0,1:T(8,128)}, u32[]{:S(2)}) copy-start(f32[512,83]{0,1:T(8,128)} %param.20) | copy-start | bytes 509956
  4.3 9.1 %copy-start.2 = (f32[512,83]{0,1:T(8,128)S(1)}, f32[512,83]{0,1:T(8,128)}, u32[]{:S(2)}) copy-start(f32[512,83]{0,1:T(8,128)} %param.21) | copy-start | bytes 509956
  5.2 9.2 %copy-start.3 = (bf16[512,83]{0,1:T(8,128)(2,1)S(1)}, bf16[512,83]{0,1:T(8,128)(2,1)}, u32[]{:S(2)}) copy-start(bf16[512,83]{0,1:T(8,128)(2,1)} %param.39) | copy-start | bytes 254980
  5.2 9.3 %copy-start = (bf16[16,128,512]{2,1,0:T(8,128)(2,1)}, bf16[16,128,512]{2,1,0:T(8,128)(2,1)S(1)}, u32[]{:S(2)}) copy-start(bf16[16,128,512]{2,1,0:T(8,128)(2,1)S(1)} %bitcast_dynamic-update-slice_fusion.wpad) | copy-start | bytes 6291460

commit v2 on v1

v2 whole, which is shorter than its diff:
```python
import functools
import math

import jax
import jax.numpy as jnp
from jax import lax
from jax.experimental import pallas as pl
from jax.experimental.pallas import tpu as pltpu
from jax.sharding import PartitionSpec as P

F32 = jnp.float32
BF16 = jnp.bfloat16
LANES = 128
EDGE_KINDS = 6


def chip_ring(side):
    order = list(range(side))
    for y in range(1, side):
        columns = range(1, side)
        order += [y * side + x for x in (reversed(columns) if y % 2 else columns)]
    order += [y * side for y in range(side - 1, 0, -1)]
    return order


def dot(left, right):
    return jnp.dot(left, right, preferred_element_type=F32)


def silu(values):
    half = 0.5 * values
    return half + half * jnp.tanh(half)


def layer_norm(values):
    centred = values - jnp.mean(values, axis=-1, keepdims=True)
    spread = jnp.mean(centred * centred, axis=-1, keepdims=True)
    return centred * lax.rsqrt(spread + 1e-5)


def tail(pre_act, w_second):
    return layer_norm(dot(silu(pre_act).astype(BF16), w_second))


def pick(index, table):
    found = jnp.int32(0)
    for position, value in enumerate(table):
        found = found + jnp.where(index == position, jnp.int32(value), jnp.int32(0))
    return found


def rows_mod(shape, modulus):
    return lax.broadcasted_iota(jnp.int32, shape, 0) & (modulus - 1)


def next_quarter(values):
    rows = values.shape[0]
    return jnp.where(rows_mod(values.shape, 4) < 3, pltpu.roll(values, rows - 1, 0), pltpu.roll(values, 3, 0))


def prev_quarter(values):
    rows = values.shape[0]
    return jnp.where(rows_mod(values.shape, 4) > 0, pltpu.roll(values, 1, 0), pltpu.roll(values, rows - 3, 0))


def kernel(cfg, xp_h, xc_h, frc_in, fix_in, m2g_in, g2m_in, mef_in, mft_in, ns_in, wpad, wfin, wembed_h, win_h, wout_h, nin_h, nout_h, wself_h, whid_h,
           out_a, out_b,
           xbuf, tbuf, nat, mt, gf_in, mf_in, wembed, win, wout, nin, nout, wself, whid, state, perm, mf_next, mf_all, mf_blk,
           fst_s, fst_r, stage_s, stage_r, back_s, back_r, mesh_buf, halo,
           edges, edge_base, mesh_lat, g2m_lat, m2g_lat, grid_lat, grid_cur,
           enc_base, enc_node, dec_base, dec_static, dec_node, mesh_band,
           proj, recv, node_pre, acc, pre_ref, far,
           misc_sem, wl_sem, shift_sem, fst_ss, fst_rs, stg_ss, stg_rs, bck_ss, bck_rs, halo_ss, halo_rs):
    group, ring, latent, ratio, layers, half = cfg
    chips = len(ring)
    mesh_dev = 2 * half
    grid_dev = ratio * mesh_dev
    chunk = grid_dev // 2
    devices = [2 * ring[q // 2] + q % 2 for q in range(group)]
    me = lax.axis_index("gp")
    core = me % 2
    where_of = [0] * chips
    for position, chip in enumerate(ring):
        where_of[chip] = position
    chip_place = pick(me // 2, where_of)
    place = 2 * chip_place + core
    up = jnp.where(core == 0, me + 1, 2 * pick(chip_place, ring[1:] + ring[:1]))
    down = jnp.where(core == 1, me - 1, 2 * pick(chip_place, ring[-1:] + ring[:-1]) + 1)

    def target(index):
        return dict(device_id={"gp": index}, device_id_type=pl.DeviceIdType.MESH)

    def local(source, dest, sem):
        return pltpu.make_async_copy(source, dest, sem)

    def block_copies(block, slot):
        return [local(win_h.at[block], win.at[slot], wl_sem.at[slot, 0]), local(wout_h.at[block], wout.at[slot], wl_sem.at[slot, 1]),
                local(nin_h.at[block], nin.at[slot], wl_sem.at[slot, 2]), local(nout_h.at[block], nout.at[slot], wl_sem.at[slot, 3])]

    x_copies = [local(xp_h, xbuf.at[0], misc_sem.at[3]), local(xc_h, xbuf.at[1], misc_sem.at[4])]
    embed_copy = local(wembed_h, wembed, misc_sem.at[0])
    self_copy = local(wself_h, wself, misc_sem.at[1])
    hid_copy = local(whid_h, whid, misc_sem.at[2])
    enc_copies = block_copies(0, 2)
    dec_copies = block_copies(layers + 1, 3)
    for copy in [embed_copy] + x_copies + enc_copies + [self_copy] + dec_copies + [hid_copy] + block_copies(1, 0):
        copy.start()

    barrier = pltpu.get_barrier_semaphore()
    for hop in range(1, group):
        pl.semaphore_signal(barrier, inc=1, **target(lax.rem(me + hop, group)))

    row = lax.broadcasted_iota(jnp.int32, (mesh_dev, mesh_dev), 0)
    col = lax.broadcasted_iota(jnp.int32, (mesh_dev, mesh_dev), 1)

    def by_target(index):
        return ((index >> 1) & 1) * half + (index >> 2) * 2 + (index & 1)

    def by_source(index):
        b = (index >> 2) & 15
        return ((index & 3) * 8 + (b >> 1)) * 4 + (b & 1) * 2 + (index >> 6)

    for slot, mask in enumerate((by_target(row) == col, by_source(row) == col, row == by_source(col), row == by_target(col))):
        perm[slot] = jnp.where(mask, 1.0, 0.0).astype(BF16)

    for ref in (enc_base, enc_node, dec_base, dec_node, dec_static, acc, proj, recv, node_pre, pre_ref, far, state, tbuf, mt):
        ref[...] = jnp.zeros_like(ref)
    def halves():
        return [(part * chunk, (part + 1) * chunk) for part in range(2)]

    steps, force = frc_in.shape[1], frc_in.shape[0]
    fixed, efeat = fix_in.shape[0], m2g_in.shape[0]
    for f in range(force):
        for which in range(steps):
            tbuf[which * force + f:which * force + f + 1] = frc_in[f, which:which + 1]
    at = steps * force
    tbuf[at:at + fixed] = fix_in[...]
    at += fixed
    tbuf[at:at + efeat] = m2g_in[...]
    at += efeat
    tbuf[at:at + efeat] = g2m_in[...]
    nat[...] = tbuf[...].T
    for k in range(EDGE_KINDS):
        mt[k * efeat:(k + 1) * efeat] = mef_in[k]
    base = EDGE_KINDS * efeat
    mt[base:base + mft_in.shape[0]] = mft_in[...]
    base += mft_in.shape[0]
    turned = mt[...].T
    lane = lax.broadcasted_iota(jnp.int32, turned.shape, 1)
    for r in range(ratio):
        rows = nat[pl.ds(r, mesh_dev, stride=ratio), :]
        gf_in[r * mesh_dev:(r + 1) * mesh_dev] = rows.astype(BF16)
        first = base + r * efeat
        turned = jnp.where(jnp.logical_and(lane >= first, lane < first + efeat), pltpu.roll(rows, first - at, 1), turned)
    mf_in[...] = turned.astype(BF16)
    tbuf[...] = jnp.zeros_like(tbuf)
    embed_copy.wait()
    for lo, hi in halves()[:1]:
        m2g_lat[lo:hi] = tail(dot(gf_in[lo:hi], wpad[4]), wembed[3]).astype(BF16)
    pl.semaphore_wait(barrier, group - 1)
    shift = pltpu.make_async_remote_copy(mf_in.at[pl.ds(0, half)], mf_next, shift_sem.at[0], shift_sem.at[1],
                                         **target(lax.rem(me + group - 1, group)))
    shift.start()

    def exchange(src, dst, send_sem, recv_sem, slot, dest_of, source_of):
        copies = []
        for part in range(group):
            dest = dest_of(part)
            copy = pltpu.make_async_remote_copy(src.at[part], dst.at[slot], send_sem.at[part], recv_sem.at[slot], **target(dest))
            copies.append((dest, copy))

            @pl.when(dest != me)
            def _(copy=copy):
                copy.start()

            @pl.when(dest == me)
            def _(part=part):
                dst[slot] = src[part]

        def finish():
            for part in range(group):
                @pl.when(source_of(part) != me)
                def _(part=part):
                    pltpu.make_async_remote_copy(src.at[part], dst.at[part], send_sem.at[part], recv_sem.at[part], **target(up)).wait_recv()

            for dest, copy in copies:
                @pl.when(dest != me)
                def _(copy=copy):
                    copy.wait_send()
        return finish

    def forth(src, dst, send_sem, recv_sem):
        return exchange(src, dst, send_sem, recv_sem, me, lambda q: devices[q], lambda d: d)

    def back(src, dst, send_sem, recv_sem):
        return exchange(src, dst, send_sem, recv_sem, place, lambda d: d, lambda q: devices[q])

    for lo, hi in halves()[1:]:
        m2g_lat[lo:hi] = tail(dot(gf_in[lo:hi], wpad[4]), wembed[3]).astype(BF16)
    for copy in x_copies:
        copy.wait()
    for which in range(2):
        tbuf[:xbuf.shape[1]] = xbuf[which]
        nat[...] = tbuf[...].T
        for r in range(ratio):
            state[which, r * mesh_dev:(r + 1) * mesh_dev] = nat[pl.ds(r, mesh_dev, stride=ratio), :]
    shift.wait()
    mf_all[:half] = mf_in[half:]
    mf_all[half:] = mf_next[...]
    feats = mf_all[...]
    fst_s[...] = dot(perm[0], feats).astype(BF16).reshape(fst_s.shape)
    fst_done = forth(fst_s, fst_r, fst_ss, fst_rs)
    mesh_lat[...] = tail(dot(feats, wpad[5 + EDGE_KINDS]), wembed[1]).astype(BF16)
    for copy in enc_copies:
        copy.wait()
    recv[...] = dot(mesh_lat[...], win[2, 2 * latent:])
    enc_node[...] = dot(mesh_lat[...], nin[2, :latent])
    for r in range(ratio):
        dec_base[r * mesh_dev:(r + 1) * mesh_dev] = dot(feats, wpad[6 + EDGE_KINDS + r])
    for lo, hi in halves():
        g2m_lat[lo:hi] = tail(dec_base[lo:hi], wembed[2]).astype(BF16)
    for lo, hi in halves():
        dec_node[lo:hi] = dot(g2m_lat[lo:hi], win[2, :latent])
    for r in range(ratio):
        rows = slice(r * mesh_dev, (r + 1) * mesh_dev)
        enc_base[rows] = dec_node[rows] + recv[...]
    for copy in dec_copies:
        copy.wait()
    for lo, hi in halves():
        dec_static[lo:hi] = dot(m2g_lat[lo:hi], win[3, :latent])
    self_copy.wait()
    hid_copy.wait()

    top, low_end = 4 * mesh_dev, 5 * mesh_dev
    near_index, far_index = core, 1 - core
    side_row = lax.broadcasted_iota(jnp.int32, (half, latent), 0)

    def step_up(values):
        moved = pltpu.roll(values, half - 4, 0)
        return jnp.where(side_row >= half - 4, next_quarter(moved), moved)

    def step_down(values):
        moved = pltpu.roll(values, 4, 0)
        return jnp.where(side_row < 4, prev_quarter(moved), moved)

    def run_layer(step, layer):
        slot = layer % 2
        later = 1 - slot

        def send(part, dest):
            return pltpu.make_async_remote_copy(mesh_buf.at[slot, pl.ds(part * half, half)], halo.at[slot, part],
                                                halo_ss.at[slot, part], halo_rs.at[slot, part], **target(dest))
        to_down, to_up = send(0, down), send(1, up)

        @pl.when(core == 0)
        def _():
            to_down.start()
            to_up.start()

        @pl.when(core == 1)
        def _():
            to_up.start()
            to_down.start()

        for copy in block_copies(layer + 1, slot):
            copy.wait()

        @pl.when(jnp.logical_or(step == 0, layer < layers - 1))
        def _():
            for copy in block_copies(1 + (layer + 1) % layers, later):
                copy.start()

        @pl.when(layer == 0)
        def _():
            edges[...] = edge_base[...]

        w_edge = win.at[slot]
        w_edge_two = wout.at[slot]
        w_node = nin.at[slot]
        w_node_two = nout.at[slot]
        nodes = mesh_buf[slot]
        proj[...] = dot(nodes, w_edge[latent:2 * latent])
        recv[...] = dot(nodes, w_edge[2 * latent:])
        pre_ref[...] = dot(edges[...], w_edge[:latent])

        def renew(lo, rows, sent):
            hidden = silu(pre_ref[lo:lo + sent.shape[0]] + sent + rows).astype(BF16)
            return hidden

        everyone = recv[...]
        hidden_a = jnp.concatenate([
            renew(2 * mesh_dev, everyone, next_quarter(proj[...])),
            renew(3 * mesh_dev, everyone, prev_quarter(proj[...])),
            renew(top, everyone, jnp.concatenate([proj[half:], proj[:half]], axis=0))], axis=0)
        out_a_rows = dot(hidden_a, w_edge_two[...])
        hidden_b = jnp.concatenate([
            renew(0, everyone, jnp.concatenate([step_up(proj[:half]), step_up(proj[half:])], axis=0)),
            renew(mesh_dev, everyone, jnp.concatenate([step_down(proj[:half]), step_down(proj[half:])], axis=0))], axis=0)
        out_b_rows = dot(hidden_b, w_edge_two[...])
        node_pre[...] = dot(nodes, w_node[:latent])

        def settle(lo, values, first=False):
            new = (edges[lo:lo + mesh_dev].astype(F32) + layer_norm(values)).astype(BF16)
            edges[lo:lo + mesh_dev] = new
            acc[...] = new.astype(F32) if first else acc[...] + new.astype(F32)

        settle(2 * mesh_dev, out_a_rows[:mesh_dev], first=True)
        settle(3 * mesh_dev, out_a_rows[mesh_dev:2 * mesh_dev])
        settle(top, out_a_rows[2 * mesh_dev:])
        settle(0, out_b_rows[:mesh_dev])
        settle(mesh_dev, out_b_rows[mesh_dev:])

        def side(index, sent):
            lo = pl.multiple_of(low_end + index * half, half)
            into = pl.multiple_of((1 - index) * half, half)
            pre = pre_ref[pl.ds(lo, half)] + sent + recv[pl.ds(into, half)]
            new = (edges[pl.ds(lo, half)].astype(F32) + tail(pre, w_edge_two[...])).astype(BF16)
            edges[pl.ds(lo, half)] = new
            acc[pl.ds(into, half)] = acc[pl.ds(into, half)] + new.astype(F32)

        def arrived(index):
            pltpu.make_async_remote_copy(mesh_buf.at[slot, pl.ds(0, half)], halo.at[slot, index],
                                         halo_ss.at[slot, index], halo_rs.at[slot, index], **target(up)).wait_recv()

        arrived(near_index)
        far[...] = dot(halo[slot, near_index], w_edge[latent:2 * latent])
        side(near_index, far[...])
        arrived(far_index)
        far[...] = dot(halo[slot, far_index], w_edge[latent:2 * latent])
        sent = far[...]
        sent = jnp.where(place == group - 1, step_up(sent), jnp.where(place == 0, step_down(sent), sent))
        side(far_index, sent)
        update = tail(node_pre[...] + dot(acc[...].astype(BF16), w_node[latent:]), w_node_two[...])
        to_down.wait_send()
        to_up.wait_send()
        mesh_buf[later] = (nodes.astype(F32) + update).astype(BF16)

    mean, spread, diff_mean, diff_spread = ns_in[0:1], ns_in[1:2], ns_in[2:3], ns_in[3:4]

    def run_step(step):
        after = lax.rem(step + 2, 3)
        for lo, hi in halves():
            past = ((state[step, lo:hi] - mean) / spread).astype(BF16)
            now = ((state[step + 1, lo:hi] - mean) / spread).astype(BF16)
            pre = dot(past, wpad[0]) + dot(now, wpad[1]) + dot(gf_in[lo:hi], wpad[2 + step])
            grid_lat[lo:hi] = tail(pre, wembed[0]).astype(BF16)
        for part, (lo, hi) in enumerate(halves()):
            pre = enc_base[lo:hi] + dot(grid_lat[lo:hi], win[2, latent:2 * latent])
            new = (g2m_lat[lo:hi].astype(F32) + tail(pre, wout[2])).astype(BF16).astype(F32)
            total = new[:mesh_dev] + new[mesh_dev:]
            acc[...] = total if part == 0 else acc[...] + total
        update = tail(enc_node[...] + dot(acc[...].astype(BF16), nin[2, latent:]), nout[2])
        mesh_band[...] = (mesh_lat[...].astype(F32) + update).astype(BF16)
        stage_s[...] = dot(perm[0], mesh_band[...]).astype(BF16).reshape(stage_s.shape)
        arrive = forth(stage_s, stage_r, stg_ss, stg_rs)
        for lo, hi in halves():
            lat = grid_lat[lo:hi]
            grid_cur[lo:hi] = (lat.astype(F32) + tail(dot(lat, wself[0]), wself[1])).astype(BF16)

        @pl.when(step == 0)
        def _():
            fst_done()
            mf_blk[...] = dot(perm[1], fst_r[...].reshape(mesh_dev, LANES)).astype(BF16)
            for k in range(2, EDGE_KINDS):
                pre_ref[(k - 2) * mesh_dev:(k - 1) * mesh_dev] = dot(mf_blk[...], wpad[5 + k])
            pre_ref[top:top + half] = dot(mf_blk[:half], wpad[5])
            pre_ref[top + half:low_end] = dot(mf_blk[half:], wpad[6])
            pre_ref[low_end:low_end + half] = dot(mf_blk[half:], wpad[5])
            pre_ref[low_end + half:] = dot(mf_blk[:half], wpad[6])
            for lo in range(0, EDGE_KINDS * mesh_dev, chunk):
                edge_base[lo:lo + chunk] = tail(pre_ref[lo:lo + chunk], wembed[4]).astype(BF16)

        arrive()
        mesh_buf[0] = dot(perm[1], stage_r[...].reshape(mesh_dev, latent)).astype(BF16)

        @pl.loop(0, layers)
        def _(layer):
            run_layer(step, layer)

        back_s[...] = dot(perm[2], mesh_buf[layers % 2]).astype(BF16).reshape(back_s.shape)
        arrive = back(back_s, back_r, bck_ss, bck_rs)
        for lo, hi in halves():
            dec_base[lo:hi] = dec_static[lo:hi] + dot(grid_cur[lo:hi], win[3, 2 * latent:])
            dec_node[lo:hi] = dot(grid_cur[lo:hi], nin[3, :latent])
        arrive()
        mesh_band[...] = dot(perm[3], back_r[...].reshape(mesh_dev, latent)).astype(BF16)
        recv[...] = dot(mesh_band[...], win[3, latent:2 * latent])
        for lo, hi in halves():
            pre = dec_base[lo:hi] + jnp.concatenate([recv[...], recv[...]], axis=0)
            dec_edge = (m2g_lat[lo:hi].astype(F32) + tail(pre, wout[3])).astype(BF16)
            update = tail(dec_node[lo:hi] + dot(dec_edge, nin[3, latent:]), nout[3])
            grid_out = (grid_cur[lo:hi].astype(F32) + update).astype(BF16)
            hidden = silu(dot(grid_out, whid[...])).astype(BF16)
            state[after, lo:hi] = state[step + 1, lo:hi] + diff_spread * lax.dot_general(hidden, wfin[...], (((1,), (1,)), ((), ())), preferred_element_type=F32) + diff_mean
        for r in range(ratio):
            nat[pl.ds(r, mesh_dev, stride=ratio), :] = state[after, r * mesh_dev:(r + 1) * mesh_dev]
        tbuf[...] = nat[...].T

        @pl.when(step == 0)
        def _():
            out_a[...] = tbuf[:out_a.shape[0]]

        @pl.when(step == 1)
        def _():
            out_b[...] = tbuf[:out_b.shape[0]]

    @pl.loop(0, 2)
    def _(step):
        run_step(step)


def solution(mesh):
    group = mesh.shape["gp"]
    side = math.isqrt(group // 2)
    ring = chip_ring(side)
    row_spec = P(("dp", "gp"))
    edge_spec = P(("dp", "gp"), None, None)
    whole = P()

    def local_run(x_prev, x_cur, forcing, grid_static, g2m_feat, m2g_feat, mesh_feat, mesh_edge_feat, norm_stats, w_grid_in, w_mesh_in, w_eemb_in, w_embed_out, w_edge_in, w_edge_out, w_node_in, w_node_out, w_grid_self, w_out_hidden, w_out_final):
        grid_dev, variables = x_prev.shape
        mesh_dev = mesh_feat.shape[0]
        ratio = grid_dev // mesh_dev
        latent = w_embed_out.shape[-1]
        layers = w_edge_in.shape[0] - 2
        steps, force = forcing.shape[1:]
        fixed = grid_static.shape[1]
        efeat = m2g_feat.shape[1]
        assert side * side * 2 == group and mesh_dev == 8 * len(ring) and mesh_dev == 128 and ratio == 4 and layers % 2 == 0

        def lanes(values, fill=0):
            return jnp.pad(values, [(0, 0)] * (values.ndim - 1) + [(0, LANES - values.shape[-1])], constant_values=fill)

        kinds = mesh_edge_feat.shape[1]
        ns = jnp.stack([lanes(norm_stats[0]), lanes(norm_stats[1], 1), lanes(norm_stats[2]), lanes(norm_stats[3])])

        def placed(*pieces):
            total = 0
            for start, rows in pieces:
                total = total + jnp.pad(rows, ((start, LANES - start - rows.shape[0]), (0, 0)))
            return total

        w_force = w_grid_in[2 * variables:2 * variables + force]
        w_fixed = w_grid_in[2 * variables + force:]
        start = steps * force
        pads = [placed((0, w_grid_in[:variables])), placed((0, w_grid_in[variables:2 * variables])),
                placed((0, w_force), (start, w_fixed)), placed((force, w_force), (start, w_fixed)),
                placed((start + fixed, w_eemb_in[1]))]
        pads += [placed((k * efeat, w_eemb_in[2])) for k in range(kinds)]
        pads += [placed((kinds * efeat, w_mesh_in))]
        pads += [placed((kinds * efeat + mesh_feat.shape[1] + r * efeat, w_eemb_in[0])) for r in range(ratio)]
        wpad = jnp.stack(pads)
        wfin = jnp.pad(w_out_final.T, ((0, LANES - variables), (0, 0)))

        vmem = pl.BlockSpec(memory_space=pltpu.VMEM)
        hbm = pl.BlockSpec(memory_space=pl.ANY)
        VM = pltpu.VMEM
        DMA = pltpu.SemaphoreType.DMA
        grid_shape = (grid_dev, latent)
        node_shape = (mesh_dev, latent)
        part_shape = (group, mesh_dev // group, latent)
        feat_shape = part_shape[:2] + (LANES,)
        edge_shape = (EDGE_KINDS * mesh_dev, latent)
        half = mesh_dev // 2
        scratch = [
            VM((2, variables, grid_dev), F32), VM((LANES, grid_dev), F32), VM((grid_dev, LANES), F32), VM((LANES, mesh_dev), F32), VM((grid_dev, LANES), BF16), VM((mesh_dev, LANES), BF16),
            VM(w_embed_out.shape, BF16), VM((4,) + w_edge_in.shape[1:], BF16), VM((4,) + w_edge_out.shape[1:], BF16),
            VM((4,) + w_node_in.shape[1:], BF16), VM((4,) + w_node_out.shape[1:], BF16), VM(w_grid_self.shape, BF16), VM(w_out_hidden.shape, BF16),
            VM((3, grid_dev, LANES), F32), VM((4, mesh_dev, mesh_dev), BF16),
            VM((half, LANES), BF16), VM((mesh_dev, LANES), BF16), VM((mesh_dev, LANES), BF16),
            VM(feat_shape, BF16), VM(feat_shape, BF16), VM(part_shape, BF16), VM(part_shape, BF16), VM(part_shape, BF16), VM(part_shape, BF16),
            VM((2,) + node_shape, BF16), VM((2, 2, half, latent), BF16),
            VM(edge_shape, BF16), VM(edge_shape, BF16), VM(node_shape, BF16),
            VM(grid_shape, BF16), VM(grid_shape, BF16), VM(grid_shape, BF16), VM(grid_shape, BF16),
            VM(grid_shape, F32), VM(node_shape, F32), VM(grid_shape, F32), VM(grid_shape, F32), VM(grid_shape, F32), VM(node_shape, BF16),
            VM(node_shape, F32), VM(node_shape, F32), VM(node_shape, F32), VM(node_shape, F32), VM(edge_shape, F32), VM((half, latent), F32),
            DMA((5,)), DMA((4, 4)), DMA((2,)), DMA((group,)), DMA((group,)), DMA((group,)), DMA((group,)), DMA((group,)), DMA((group,)), DMA((2, 2)), DMA((2, 2)),
        ]
        cfg = (group, ring, latent, ratio, layers, mesh_dev // 2)
        next_t, after_t = pl.pallas_call(
            functools.partial(kernel, cfg),
            out_shape=(jax.ShapeDtypeStruct((variables, grid_dev), F32),) * 2,
            in_specs=[hbm] * 2 + [vmem] * 9 + [hbm] * 7,
            out_specs=(vmem, vmem),
            scratch_shapes=scratch,
            compiler_params=pltpu.CompilerParams(collective_id=0, has_side_effects=True, vmem_limit_bytes=60 * 1024 * 1024),
        )(x_prev.T, x_cur.T, forcing.transpose(2, 1, 0), grid_static.T, m2g_feat.T, g2m_feat.T, mesh_edge_feat.transpose(1, 2, 0), mesh_feat.T, ns, wpad, wfin,
          w_embed_out, w_edge_in, w_edge_out, w_node_in, w_node_out, w_grid_self, w_out_hidden)
        return next_t.T, after_t.T

    in_specs = (row_spec, row_spec, edge_spec, row_spec, row_spec, row_spec, row_spec, edge_spec, whole) + (whole,) * 11
    return jax.shard_map(local_run, mesh=mesh, in_specs=in_specs, out_specs=(row_spec, row_spec), check_vma=False)
```

time: 213 us -> 194 us (0.911)
  Pallas kernels: 194 us -> 183 us
  local copies, waits for them, and re-layouts: 15.1 us -> 8.69 us
    pallas_call x1, Pallas kernels: 194 us -> 183 us  [local_run(): pl.pallas_call(functools.partial(kernel, cfg), out_shape=(jax.ShapeDtypeS...]
    concatenate x6 -> x0, local copies, waits for them, and re-layouts: 4.45 us -> none  [local_run(): jnp.concatenate([forcing.reshape(grid_dev, steps * force), grid_static, m...]
    pallas_call x2 -> x0, local copies, waits for them, and re-layouts: 3.51 us -> none  [local_run(): pl.pallas_call(functools.partial(kernel, cfg), out_shape=(jax.ShapeDtypeS...]
    unnamed x37 -> x18, local copies, waits for them, and re-layouts: 2.76 us -> 4.68 us
where the time goes in v2:
time: 194 us
  Pallas kernels  183 us (94%)
  local copies, waits for them, and re-layouts  8.69 us (4%)
    pallas_call x1, Pallas kernels, local_run(): pl.pallas_call(functools.partial(kernel, cfg), out_shape=(jax.ShapeDtypeS...  183 us
    unnamed x18, local copies, waits for them, and re-layouts  4.68 us

profile of v2, /device:TPU:97, one launch (start us, length us, event | category | flops | bytes accessed | tf_op | source)
XLA Modules:
  0.0 194.0 jit_solution(1481759114432058221)
XLA Ops:
  0.6 0.0 copy-start.1
  0.6 0.8 slice_bitcast_fusion.6
  1.5 0.6 pad_maximum_fusion.ns_in
  2.1 1.0 bitcast_dynamic-update-slice_fusion.13
  3.1 0.9 slice.47
  4.0 0.8 fusion.4
  4.8 0.7 slice_bitcast_fusion
  5.7 0.7 bitcast_dynamic-update-slice_fusion.4
  6.5 0.0 copy-start
  6.5 0.0 copy-done.1
  6.5 0.7 pad.105.wfin
  7.2 0.6 copy-done
  7.9 183.0 %shard_map.203 = (f32[83,512]{1,0:T(8,128)}, f32[83,512]{1,0:T(8,128)}) custom-call(f32[83,512]{1,0:T(8,128)} %bitcast.69, f32[83,512]{1,0:T(8,128)} %bitcast.70, f32[5,2,512]{2,1,0:T(2,128)} %bitcast.74, f32[5,512]{1,0:T(8,128)} %bitcast.75, f32[4,512]{1,0:T(4,128)} %bitcast.77, f32[4,512]{1,0:T(4,128)} %bitcast.78, f32[6,4,128]{2,1,0:T(4,128)} %bitcast.76, ...), custom_call_target="tpu_custom_call" | custom-call | tf_op jit(solution)/shard_map/pallas_call | solution.py:480
  190.8 1.6 copy.39
  192.4 1.6 copy.40
  (16 shorter events, 0.2 us)
Async XLA Ops:
  0.6 5.9 %copy-start.1 = (bf16[512,83]{0,1:T(8,128)(2,1)S(1)}, bf16[512,83]{0,1:T(8,128)(2,1)}, u32[]{:S(2)}) copy-start(bf16[512,83]{0,1:T(8,128)(2,1)} %param.39) | copy-start | bytes 254980
  6.5 1.4 copy-start

commit v3 on v2

--- a/solution.py
+++ b/solution.py
@@ -233,15 +233,17 @@
 
     top, low_end = 4 * mesh_dev, 5 * mesh_dev
     near_index, far_index = core, 1 - core
-    side_row = lax.broadcasted_iota(jnp.int32, (half, latent), 0)
+    low = lax.broadcasted_iota(jnp.int32, (8, latent), 0) < 4
 
     def step_up(values):
         moved = pltpu.roll(values, half - 4, 0)
-        return jnp.where(side_row >= half - 4, next_quarter(moved), moved)
+        last = moved[half - 8:]
+        return jnp.concatenate([moved[:half - 8], jnp.where(low, last, next_quarter(last))], axis=0)
 
     def step_down(values):
         moved = pltpu.roll(values, 4, 0)
-        return jnp.where(side_row < 4, prev_quarter(moved), moved)
+        first = moved[:8]
+        return jnp.concatenate([jnp.where(low, prev_quarter(first), first), moved[8:]], axis=0)
 
     def run_layer(step, layer):
         slot = layer % 2

time: 194 us -> 194 us (level)
  no operation moved by 1% of the time
where the time goes in v3:
time: 194 us
  Pallas kernels  183 us (94%)
  local copies, waits for them, and re-layouts  8.69 us (4%)
    pallas_call x1, Pallas kernels, local_run(): pl.pallas_call(functools.partial(kernel, cfg), out_shape=(jax.ShapeDtypeS...  183 us
    unnamed x18, local copies, waits for them, and re-layouts  4.68 us

profile of v3, /device:TPU:97, one launch (start us, length us, event | category | flops | bytes accessed | tf_op | source)
XLA Modules:
  0.0 194.0 jit_solution(6146749727400314813)
XLA Ops:
  0.6 0.0 copy-start.1
  0.6 0.8 slice_bitcast_fusion.6
  1.5 0.6 pad_maximum_fusion.ns_in
  2.1 1.0 bitcast_dynamic-update-slice_fusion.13
  3.1 0.9 slice.47
  4.0 0.8 fusion.4
  4.8 0.7 slice_bitcast_fusion
  5.7 0.7 bitcast_dynamic-update-slice_fusion.4
  6.5 0.0 copy-start
  6.5 0.0 copy-done.1
  6.5 0.7 pad.105.wfin
  7.2 0.6 copy-done
  7.9 182.9 %shard_map.203 = (f32[83,512]{1,0:T(8,128)}, f32[83,512]{1,0:T(8,128)}) custom-call(f32[83,512]{1,0:T(8,128)} %bitcast.69, f32[83,512]{1,0:T(8,128)} %bitcast.70, f32[5,2,512]{2,1,0:T(2,128)} %bitcast.74, f32[5,512]{1,0:T(8,128)} %bitcast.75, f32[4,512]{1,0:T(4,128)} %bitcast.77, f32[4,512]{1,0:T(4,128)} %bitcast.78, f32[6,4,128]{2,1,0:T(4,128)} %bitcast.76, ...), custom_call_target="tpu_custom_call" | custom-call | tf_op jit(solution)/shard_map/pallas_call | solution.py:482
  190.8 1.6 copy.39
  192.4 1.6 copy.40
  (16 shorter events, 0.2 us)
Async XLA Ops:
  0.6 5.9 %copy-start.1 = (bf16[512,83]{0,1:T(8,128)(2,1)S(1)}, bf16[512,83]{0,1:T(8,128)(2,1)}, u32[]{:S(2)}) copy-start(bf16[512,83]{0,1:T(8,128)(2,1)} %param.39) | copy-start | bytes 254980
  6.5 1.4 copy-start
